TPU v7x, 128 devices: a whole 4x4x4 slice. The times are simulated.
128 devices in a mesh: gx: 8 (over y, x_hi), gy: 4 (over x_lo, core), gz: 4 (over z).
Axes of the slice: x: 4 (x_hi: 2, x_lo: 2; x = x_hi * 2 + x_lo), y: 4, z: 4, core: 2. Of those that a mesh axis runs over, the one named last changes fastest.
Arguments:
- right_side: float32 [64, 128, 1024], P('gx', 'gy', 'gz'), may hold values from -60 to 60
- wavenumber_sq: float32 [64, 128, 1024], P('gx', 'gy', 'gz'), may hold values from 0.3 to 1.5
- sketch_matrix: float32 [16, 64, 128, 1024], P(None, 'gx', 'gy', 'gz'), may hold values from -1.5 to 1.5
Outputs:
- solution: float32 [64, 128, 1024], P('gx', 'gy', 'gz')
- residual: float32 [64, 128, 1024], P('gx', 'gy', 'gz')
All inputs are finite; a program needn't handle non-finite values.
Results may differ from a plain program's by a relative error of at most 0.0003.
Values sent between devices are 32-bit elements; how exact they have to be, the bound alone decides.
No kernel may reach another device: no remote copies, remote signals or barrier semaphores. Data moves between devices by JAX's collectives and lax.ppermute only.
A program may use at most 64 MiB of HBM per device.

v0:
```python
import functools

import jax
import jax.numpy as jnp
from jax import lax
from jax.experimental import pallas as pl
from jax.experimental.pallas import tpu as pltpu
from jax.sharding import Mesh
from jax.sharding import PartitionSpec as P

SK = 16
SWEEPS = 3
ITERS = 3
RADIUS = 4
DEPTH = ITERS * RADIUS
BX, BY, BZ = 8, 32, 256
ROW0 = 24
ROWS = 80
LAYERS = BX + 2 * DEPTH
OWN = DEPTH
TILES = 3

VMEM = pltpu.VMEM
F32 = jnp.float32


def layer_of(part, idx):
    if part == "own":
        return OWN + idx
    if part == "twin":
        return OWN + 15 - idx
    if part == "relay":
        return OWN - 1 - idx
    if part == "outer_relay":
        return idx
    return OWN + 16 + idx


def distance(layer):
    return max(0, OWN - layer, layer - (OWN + BX - 1))


ALL_PARTS = (
    [("outer_relay", i) for i in range(4)]
    + [("relay", i) for i in range(8)]
    + [("own", i) for i in range(8)]
    + [("twin", i) for i in range(8)]
    + [("outer_twin", i) for i in range(4)]
)

FIRST = (
    [("A", ("own", i)) for i in range(8)]
    + [("A", ("twin", i)) for i in range(8)]
    + [("B", ("own", i), ("own", i + 1)) for i in (0, 2, 4, 6)]
    + [("B", ("twin", i), ("twin", i + 1)) for i in (4, 6)]
)
SECOND = (
    [("A", ("relay", i)) for i in range(8)]
    + [("B", ("relay", i), ("relay", i + 1)) for i in (0, 2)]
    + [
        ("C", ("outer_relay", 1), ("outer_relay", 2)),
        ("C", ("outer_relay", 3), ("outer_twin", 0)),
        ("C", ("outer_twin", 1), ("outer_twin", 2)),
    ]
)


def lane_plan():
    plan = {}
    place = [0, 0]
    order = sorted(ALL_PARTS, key=lambda part: distance(layer_of(*part)))
    for part in order:
        dist = distance(layer_of(*part))
        width = DEPTH - dist
        if width <= 0:
            continue
        tile = 0 if dist in (0, 1, 10, 11) else 1
        plan[part] = (tile, place[tile], width)
        place[tile] += width
    assert max(place) <= 128
    return plan


LANES = lane_plan()


def roll(value, shift, axis):
    shift = shift % value.shape[axis]
    if shift == 0:
        return value
    return pltpu.roll(value, shift, axis)


def prep_kernel(flip_ref, rhs_ref, coef_ref, out_ref):
    flip = flip_ref[0]
    for i in range(BX):
        source = jnp.where(flip == 1, BX - 1 - i, i)
        out_ref[0, i] = rhs_ref[source]
        out_ref[1, i] = 1.0 / (6.0 + coef_ref[source])


def pack_rows_kernel(slots, names, *refs):
    sources = dict(zip(names, refs))
    low_ref, high_ref = refs[len(names) :]
    sub = lax.broadcasted_iota(jnp.int32, (8, BZ), 0)
    for array in range(2):
        for slot, (kind, *parts) in enumerate(slots):
            values = []
            for tiles in ((0, 1), (3, 2)):
                tile = tiles[1] if kind == "B" else tiles[0]
                values.append([sources[p][array, i, tile * 8 : tile * 8 + 8] for p, i in parts])
            low, high = values
            if kind == "A":
                low_ref[array, slot] = low[0]
                high_ref[array, slot] = high[0]
            else:
                low_ref[array, slot] = jnp.where(sub < 4, low[0], roll(low[1], 4, 0))
                high_ref[array, slot] = jnp.where(sub >= 4, high[0], roll(high[1], 4, 0))


def row_sources(slots):
    found = {}
    for slot, (kind, *parts) in enumerate(slots):
        for at, part in enumerate(parts):
            below, above = (0, 7) if kind == "B" else (1, 6)
            found.setdefault(part, {})[below] = (slot, at)
            found.setdefault(part, {})[above] = (slot, at)
    return found


def halo_tile(message_ref, array, where, lane_tile):
    slot, rolled = where
    value = message_ref[array, slot, :, lane_tile * 128 : lane_tile * 128 + 128]
    return roll(value, 4, 0) if rolled else value


def assemble_kernel(*refs):
    names = ("own", "twin", "relay", "outer_relay", "outer_twin")
    sources = dict(zip(names, refs[:5]))
    below = (refs[5], refs[7])
    above = (refs[6], refs[8])
    ext_ref, low_ref, high_ref = refs[9:]
    first, second = row_sources(FIRST), row_sources(SECOND)
    lane = lax.broadcasted_iota(jnp.int32, (8, 128), 1)
    for array in range(2):
        for row_tile in range(8):
            packed = [[None, None], [None, None]]
            for part in ALL_PARTS:
                name, idx = part
                layer = layer_of(name, idx)
                tiles = []
                for lane_tile in range(2):
                    if 2 <= row_tile <= 5:
                        row = (row_tile - 2) * 8
                        value = sources[name][array, idx, row : row + 8, lane_tile * 128 : lane_tile * 128 + 128]
                    else:
                        message = 0 if part in first else 1
                        where = (first if message == 0 else second).get(part, {}).get(row_tile)
                        if where is None:
                            value = None
                        else:
                            side = below if row_tile < 2 else above
                            value = halo_tile(side[message], array, where, lane_tile)
                    if value is not None:
                        row = 8 + row_tile * 8
                        ext_ref[array, lane_tile, layer, row : row + 8] = value
                    tiles.append(value)
                if part in LANES and tiles[0] is not None:
                    tile, place, width = LANES[part]
                    mask = (lane >= place) & (lane < place + width)
                    low = roll(tiles[0], place, 1)
                    high = roll(tiles[1], place + width, 1)
                    for side, value in ((0, low), (1, high)):
                        old = packed[side][tile]
                        packed[side][tile] = value if old is None else jnp.where(mask, value, old)
            for tile in range(2):
                for side, out_ref in ((0, low_ref), (1, high_ref)):
                    value = packed[side][tile]
                    if value is not None:
                        out_ref[array, tile, row_tile * 8 : row_tile * 8 + 8] = value


def neighbours(ref, layer, row, tiles, lane):
    here = [ref[t, layer, row : row + 8] for t in range(TILES)]
    up = [roll(v, 127, 1) for v in here]
    down = [roll(v, 1, 1) for v in here]
    sums = []
    for t in tiles:
        total = ref[t, layer - 1, row : row + 8] + ref[t, layer + 1, row : row + 8]
        total = total + (ref[t, layer, row - 1 : row + 7] + ref[t, layer, row + 1 : row + 9])
        along = jnp.where(lane == 127, up[(t + 1) % TILES], up[t])
        along = along + jnp.where(lane == 0, down[(t + 2) % TILES], down[t])
        sums.append(total + along)
    return here, sums


def rows_of(reach):
    if reach == 0:
        return range(2, 6)
    return range(1, 7) if reach <= 8 else range(0, 8)


def main_kernel(
    flip_ref, sketch_hbm, ext_ref, below_ref, above_ref, vectors_ref, images_ref,
    vec, inv, za, zb, mid, sketch, sem,
):
    copy = pltpu.make_async_copy(sketch_hbm, sketch, sem)
    copy.start()
    flip = flip_ref[0]
    lane = lax.broadcasted_iota(jnp.int32, (8, 128), 1)

    for array, target in ((0, vec), (1, inv)):
        for part in LANES:
            tile, place, width = LANES[part]
            layer = layer_of(*part)
            for row_tile in rows_of(DEPTH) if distance(layer) <= 3 else rows_of(8):
                row = row_tile * 8
                low = roll(above_ref[array, tile, row : row + 8], -place, 1)
                high = roll(below_ref[array, tile, row : row + 8], -(place + width), 1)
                target[2, layer, row + 8 : row + 16] = jnp.where(lane < 64, low, high)

    def copy_layer(layer, _):
        for row_tile in range(8):
            row = 8 + row_tile * 8
            for t in range(2):
                value = ext_ref[0, t, layer, row : row + 8]
                scale = ext_ref[1, t, layer, row : row + 8]
                vec[t, layer, row : row + 8] = value
                inv[t, layer, row : row + 8] = scale
                za[t, layer, row : row + 8] = value * scale
            za[2, layer, row : row + 8] = vec[2, layer, row : row + 8] * inv[2, layer, row : row + 8]
        return 0

    lax.fori_loop(0, LAYERS, copy_layer, 0)

    for step in range(ITERS):
        reach = DEPTH - step * RADIUS

        def sweep(source, target, left, keep):
            def body(layer, _):
                for row_tile in rows_of(left):
                    row = 8 + row_tile * 8
                    _, sums = neighbours(source, layer, row, range(TILES), lane)
                    for t in range(TILES):
                        total = vec[t, layer, row : row + 8] + sums[t]
                        if keep:
                            mid[t, layer, row : row + 8] = total
                        target[t, layer, row : row + 8] = total * inv[t, layer, row : row + 8]
                return 0

            lax.fori_loop(OWN - left, OWN + BX + left, body, 0)

        sweep(za, zb, reach - 1, False)
        sweep(zb, za, reach - 2, False)
        sweep(za, zb, reach - 3, True)
        left = reach - 4
        last = step == ITERS - 1

        def apply(layer, _):
            for row_tile in rows_of(left):
                row = 8 + row_tile * 8
                tiles = range(2) if last else range(TILES)
                here, sums = neighbours(zb, layer, row, tiles, lane)
                for t in tiles:
                    value = 12.0 * here[t] - mid[t, layer, row : row + 8] - sums[t]
                    vec[t, layer, row : row + 8] = value
                    if not last:
                        za[t, layer, row : row + 8] = value * inv[t, layer, row : row + 8]
            return 0

        lax.fori_loop(OWN - left, OWN + BX + left, apply, 0)

        def keep_own(i, _):
            natural = jnp.where(flip == 1, BX - 1 - i, i)
            for row in range(0, BY, 8):
                for t in range(2):
                    cols = slice(t * 128, t * 128 + 128)
                    at = slice(ROW0 + row, ROW0 + row + 8)
                    vectors_ref[step + 1, natural, row : row + 8, cols] = vec[t, OWN + i, at]
                    vectors_ref[4 + step, natural, row : row + 8, cols] = zb[t, OWN + i, at]
            return 0

        if step == 0:

            def keep_first(i, _):
                natural = jnp.where(flip == 1, BX - 1 - i, i)
                for row in range(0, BY, 8):
                    for t in range(2):
                        cols = slice(t * 128, t * 128 + 128)
                        at = slice(ROW0 + row, ROW0 + row + 8)
                        vectors_ref[0, natural, row : row + 8, cols] = ext_ref[0, t, OWN + i, at]
                return 0

            lax.fori_loop(0, BX, keep_first, 0)
        lax.fori_loop(0, BX, keep_own, 0)

    copy.wait()
    group = 4
    totals = []
    for start in range(0, SK, group):

        def body(i, carry):
            carry = list(carry)
            for row in range(0, BY, 8):
                for t in range(2):
                    cols = slice(t * 128, t * 128 + 128)
                    fields = [vectors_ref[j, i, row : row + 8, cols] for j in range(4)]
                    for s in range(group):
                        weight = sketch[start + s, i, row : row + 8, cols]
                        for j in range(4):
                            carry[j * group + s] = carry[j * group + s] + weight * fields[j]
            return tuple(carry)

        zero = jnp.zeros((8, 128), F32)
        totals.append(lax.fori_loop(0, BX, body, (zero,) * (4 * group)))
    lanes = lax.broadcasted_iota(jnp.int32, (1, 128), 1)
    image = jnp.zeros((1, 128), F32)
    for g, sums in enumerate(totals):
        for j in range(4):
            for s in range(group):
                value = jnp.sum(jnp.sum(sums[j * group + s], axis=0, keepdims=True), axis=1, keepdims=True)
                image = jnp.where(lanes == j * SK + g * group + s, value, image)
    images_ref[...] = jnp.broadcast_to(image, images_ref.shape)


def dot(left, right):
    return jnp.sum(left * right, axis=0, keepdims=True)


def small_solve(totals):
    row = lax.broadcasted_iota(jnp.int32, (4 * SK, 128), 0)
    col = lax.broadcasted_iota(jnp.int32, (4 * SK, 128), 1)
    wide = jnp.where(row == col, jnp.broadcast_to(totals, (4 * SK, 128)), 0.0)
    spread = jnp.broadcast_to(jnp.sum(wide, axis=1, keepdims=True), (4 * SK, 128))
    sketches = [spread[j * SK : (j + 1) * SK] for j in range(4)]
    zero = jnp.zeros((1, 128), F32)
    beta = jnp.sqrt(dot(sketches[0], sketches[0]))
    basis = [[1.0 / beta, zero, zero, zero]]
    images = [sketches[0] / beta]
    hessen = [[zero] * ITERS for _ in range(ITERS + 1)]
    for j in range(ITERS):
        combo = [zero] + [basis[j][i] for i in range(3)]
        image = combo[1] * sketches[1]
        for i in range(1, j + 1):
            image = image + combo[i + 1] * sketches[i + 1]
        weights = [dot(member, image) for member in images]
        rest = image
        for i in range(j + 1):
            rest = rest - weights[i] * images[i]
            combo = [combo[k] - weights[i] * basis[i][k] for k in range(4)]
            hessen[i][j] = weights[i]
        length = jnp.sqrt(dot(rest, rest))
        hessen[j + 1][j] = length
        basis.append([entry / length for entry in combo])
        images.append(rest / length)
    target = [beta, zero, zero, zero]

    def inner(left, right):
        total = left[0] * right[0]
        for a, b in zip(left[1:], right[1:]):
            total = total + a * b
        return total

    members = []
    upper = [[None] * ITERS for _ in range(ITERS)]
    for j in range(ITERS):
        column = [hessen[i][j] for i in range(ITERS + 1)]
        for i in range(j):
            factor = inner(members[i], column)
            upper[i][j] = factor
            column = [c - factor * m for c, m in zip(column, members[i])]
        diag = jnp.sqrt(inner(column, column))
        upper[j][j] = diag
        members.append([c / diag for c in column])
    coeffs = [None] * ITERS
    for j in reversed(range(ITERS)):
        accum = inner(members[j], target)
        for i in range(j + 1, ITERS):
            accum = accum - upper[j][i] * coeffs[i]
        coeffs[j] = accum / upper[j][j]
    leftover = []
    for i in range(ITERS + 1):
        total = hessen[i][0] * coeffs[0]
        for j in range(1, ITERS):
            total = total + hessen[i][j] * coeffs[j]
        leftover.append(target[i] - total)
    for_images = []
    for i in range(ITERS):
        total = coeffs[0] * basis[0][i]
        for j in range(1, ITERS):
            total = total + coeffs[j] * basis[j][i]
        for_images.append(total)
    for_vectors = []
    for i in range(ITERS + 1):
        total = leftover[0] * basis[0][i]
        for j in range(1, ITERS + 1):
            total = total + leftover[j] * basis[j][i]
        for_vectors.append(total)
    return for_images, for_vectors


def final_kernel(sums_ref, vectors_ref, solution_ref, residual_ref):
    totals = jnp.sum(sums_ref[...], axis=0, keepdims=True)
    for_images, for_vectors = small_solve(totals)
    for_images = [jnp.broadcast_to(w, (8, 128)) for w in for_images]
    for_vectors = [jnp.broadcast_to(w, (8, 128)) for w in for_vectors]

    def body(i, _):
        for row in range(0, BY, 8):
            for t in range(2):
                at = (i, slice(row, row + 8), slice(t * 128, t * 128 + 128))
                total = for_images[0] * vectors_ref[(4, *at)]
                for j in range(1, ITERS):
                    total = total + for_images[j] * vectors_ref[(4 + j, *at)]
                solution_ref[at] = total
                total = for_vectors[0] * vectors_ref[(0, *at)]
                for j in range(1, ITERS + 1):
                    total = total + for_vectors[j] * vectors_ref[(j, *at)]
                residual_ref[at] = total
        return 0

    lax.fori_loop(0, BX, body, 0)


def vmem(count):
    return [pl.BlockSpec(memory_space=VMEM)] * count


SMEM_SPEC = pl.BlockSpec(memory_space=pltpu.SMEM)


def struct(*shape):
    return jax.ShapeDtypeStruct(shape, F32)


def params(mib):
    return pltpu.CompilerParams(vmem_limit_bytes=mib << 20)


def local(right_side, wavenumber_sq, sketch_matrix):
    flip = lax.axis_index("xh").astype(jnp.int32).reshape(1)
    block = pl.pallas_call(
        prep_kernel,
        out_shape=struct(2, BX, BY, BZ),
        in_specs=[SMEM_SPEC] + vmem(2),
        out_specs=vmem(1)[0],
        compiler_params=params(8),
        name="prep",
    )(flip, right_side, wavenumber_sq)

    pairs = [(y * 2 + h, (y + (1 - 2 * h)) % 4 * 2 + h) for y in range(4) for h in range(2)]
    back = [(b, a) for a, b in pairs]
    around = [(i, (i + 1) % 4) for i in range(4)]
    inverse = [(b, a) for a, b in around]
    twin = lax.ppermute(block, "xh", [(0, 1), (1, 0)])
    outer_relay = lax.ppermute(block[:, 4:], ("y", "xh"), pairs)
    outer_twin = lax.ppermute(block[:, :4], ("y", "xh"), back)
    relay = lax.ppermute(twin, ("y", "xh"), pairs)

    def pack(slots, names, *parts):
        count = len(slots)
        low, high = pl.pallas_call(
            functools.partial(pack_rows_kernel, slots, names),
            out_shape=[struct(2, count, 8, BZ)] * 2,
            in_specs=vmem(len(parts)),
            out_specs=vmem(2),
            compiler_params=params(8),
            name="pack_rows",
        )(*parts)
        above = lax.ppermute(low, ("xl", "co"), inverse)
        below = lax.ppermute(high, ("xl", "co"), around)
        return below, above

    below_1, above_1 = pack(FIRST, ("own", "twin"), block, twin)
    below_2, above_2 = pack(
        SECOND, ("relay", "outer_relay", "outer_twin"), relay, outer_relay, outer_twin
    )
    ext, low, high = pl.pallas_call(
        assemble_kernel,
        out_shape=[struct(2, 2, LAYERS, ROWS, 128), struct(2, 2, 64, 128), struct(2, 2, 64, 128)],
        in_specs=vmem(9),
        out_specs=vmem(3),
        compiler_params=params(16),
        name="assemble",
    )(block, twin, relay, outer_relay, outer_twin, below_1, above_1, below_2, above_2)
    above = lax.ppermute(low, "z", inverse)
    below = lax.ppermute(high, "z", around)

    field = VMEM((TILES, LAYERS, ROWS, 128), F32)
    vectors, images = pl.pallas_call(
        main_kernel,
        out_shape=[struct(7, BX, BY, BZ), struct(128, 128)],
        in_specs=[SMEM_SPEC, pl.BlockSpec(memory_space=pl.ANY)] + vmem(3),
        out_specs=vmem(2),
        scratch_shapes=[field] * 5 + [VMEM((SK, BX, BY, BZ), F32), pltpu.SemaphoreType.DMA],
        compiler_params=params(40),
        name="krylov",
    )(flip, sketch_matrix, ext, below, above)

    sums = lax.all_to_all(images, ("y", "xh", "xl", "co", "z"), 0, 0, tiled=True)
    return tuple(
        pl.pallas_call(
            final_kernel,
            out_shape=[struct(BX, BY, BZ)] * 2,
            in_specs=vmem(2),
            out_specs=vmem(2),
            compiler_params=params(8),
            name="combine",
        )(sums, vectors)
    )


def solution(mesh):
    finer = Mesh(mesh.devices.reshape(4, 2, 2, 2, 4), ("y", "xh", "xl", "co", "z"))
    spec = (("y", "xh"), ("xl", "co"), "z")
    return jax.shard_map(
        local,
        mesh=finer,
        in_specs=(P(*spec), P(*spec), P(None, *spec)),
        out_specs=(P(*spec), P(*spec)),
        check_vma=False,
    )
```

profile of v0, /device:TPU:1, one launch (start us, length us, event | category | flops | bytes accessed | tf_op | source)
XLA Modules:
  0.0 105.5 jit_solution(17407858018281299050)
XLA Ops:
  0.7 1.1 %copy-done.1 = f32[8,32,256]{2,1,0:T(8,128)S(1)} copy-done((f32[8,32,256]{2,1,0:T(8,128)S(1)}, f32[8,32,256]{2,1,0:T(8,128)}, u32[]{:S(2)}) %copy-start.1) | copy-done | bytes 262168
  1.7 1.2 %copy-done.2 = f32[8,32,256]{2,1,0:T(8,128)S(1)} copy-done((f32[8,32,256]{2,1,0:T(8,128)S(1)}, f32[8,32,256]{2,1,0:T(8,128)}, u32[]{:S(2)}) %copy-start.2) | copy-done | bytes 262168
  3.0 3.6 %collective-permute-start = (f32[2,8,32,256]{3,2,1,0:T(8,128)S(1)}, f32[2,8,32,256]{3,2,1,0:T(8,128)S(1)}, u32[]{:S(2)}, u32[]{:S(2)}) collective-permute-start(f32[2,8,32,256]{3,2,1,0:T(8,128)S(1)} %prep.1.refs_0_), channel_id=1, source_target_pairs={{0,16},{16,0},{1,17},{17,1},{2,18},{18,2},{3,19},{19,3},{4,20},{20... | collective-permute-start | bytes 1572872 | tf_op jit(solution)/shard_map/ppermute | solution.py:455
  6.6 11.2 %collective-permute-done.refs_1_ = f32[2,8,32,256]{3,2,1,0:T(8,128)S(1)} collective-permute-done((f32[2,8,32,256]{3,2,1,0:T(8,128)S(1)}, f32[2,8,32,256]{3,2,1,0:T(8,128)S(1)}, u32[]{:S(2)}, u32[]{:S(2)}) %collective-permute-start) | collective-permute-done | bytes 524320 | tf_op jit(solution)/shard_map/ppermute | solution.py:455
  17.9 1.6 %collective-permute-start.1 = (f32[2,8,32,256]{3,2,1,0:T(8,128)S(1)}, f32[2,8,32,256]{3,2,1,0:T(8,128)S(1)}, u32[]{:S(2)}, u32[]{:S(2)}) collective-permute-start(f32[2,8,32,256]{3,2,1,0:T(8,128)S(1)} %collective-permute-done.refs_1_), channel_id=1, source_target_pairs={{0,32},{16,112},{32,64},{48,16},{64,96},{80,48},{96,0},{112,80},{1... | collective-permute-start | bytes 1572872 | tf_op jit(solution)/shard_map/ppermute | solution.py:458
  19.5 1.5 %collective-permute-start.3 = (f32[2,4,32,256]{3,2,1,0:T(8,128)S(1)}, f32[2,4,32,256]{3,2,1,0:T(8,128)S(1)}, u32[]{:S(2)}, u32[]{:S(2)}) collective-permute-start(f32[2,4,32,256]{3,2,1,0:T(8,128)S(1)} %get-tuple-element.20), channel_id=1, source_target_pairs={{32,0},{112,16},{64,32},{16,48},{96,64},{48,80},{0,96},{80,112},{3... | collective-permute-start | bytes 786440 | tf_op jit(solution)/shard_map/ppermute | solution.py:457
  21.0 0.0 collective-permute-start.2
  21.1 0.1 pack_rows.2
  21.1 3.5 %collective-permute-start.4 = (f32[2,22,8,256]{3,2,1,0:T(8,128)S(1)}, f32[2,22,8,256]{3,2,1,0:T(8,128)S(1)}, u32[]{:S(2)}, u32[]{:S(2)}) collective-permute-start(f32[2,22,8,256]{3,2,1,0:T(8,128)S(1)} %get-tuple-element.11), channel_id=1, source_target_pairs={{0,4},{4,8},{8,12},{12,0},{1,5},{5,9},{9,13},{13,1},{2,6},{6,10},{... | collective-permute-start | bytes 1081352 | tf_op jit(solution)/shard_map/ppermute | solution.py:471
  24.6 0.0 collective-permute-start.5
  24.7 1.0 collective-permute-done.3.refs_2_.refs_4_
  25.6 11.7 %collective-permute-done.2.refs_1_.refs_3_ = f32[2,4,32,256]{3,2,1,0:T(8,128)S(1)} collective-permute-done((f32[2,4,32,256]{3,2,1,0:T(8,128)S(1)}, f32[2,4,32,256]{3,2,1,0:T(8,128)S(1)}, u32[]{:S(2)}, u32[]{:S(2)}) %collective-permute-start.2) | collective-permute-done | bytes 262176 | tf_op jit(solution)/shard_map/ppermute | solution.py:456
  37.3 0.0 collective-permute-done.1.refs_0_.refs_2_
  37.3 3.3 %collective-permute-start.6 = (f32[2,13,8,256]{3,2,1,0:T(8,128)S(1)}, f32[2,13,8,256]{3,2,1,0:T(8,128)S(1)}, u32[]{:S(2)}, u32[]{:S(2)}) collective-permute-start(f32[2,13,8,256]{3,2,1,0:T(8,128)S(1)} %get-tuple-element.13), channel_id=1, source_target_pairs={{0,4},{4,8},{8,12},{12,0},{1,5},{5,9},{9,13},{13,1},{2,6},{6,10},{... | collective-permute-start | bytes 638984 | tf_op jit(solution)/shard_map/ppermute | solution.py:471
  40.6 0.0 collective-permute-start.7
  40.6 4.2 %collective-permute-done.6.refs_7_ = f32[2,13,8,256]{3,2,1,0:T(8,128)S(1)} collective-permute-done((f32[2,13,8,256]{3,2,1,0:T(8,128)S(1)}, f32[2,13,8,256]{3,2,1,0:T(8,128)S(1)}, u32[]{:S(2)}, u32[]{:S(2)}) %collective-permute-start.6) | collective-permute-done | bytes 213024 | tf_op jit(solution)/shard_map/ppermute | solution.py:471
  44.9 1.5 %collective-permute-done.7.refs_8_ = f32[2,13,8,256]{3,2,1,0:T(8,128)S(1)} collective-permute-done((f32[2,13,8,256]{3,2,1,0:T(8,128)S(1)}, f32[2,13,8,256]{3,2,1,0:T(8,128)S(1)}, u32[]{:S(2)}, u32[]{:S(2)}) %collective-permute-start.7) | collective-permute-done | bytes 213024 | tf_op jit(solution)/shard_map/ppermute | solution.py:470
  46.4 0.9 assemble.1
  47.3 1.7 %collective-permute-start.8 = (f32[2,2,64,128]{3,2,1,0:T(8,128)S(1)}, f32[2,2,64,128]{3,2,1,0:T(8,128)S(1)}, u32[]{:S(2)}, u32[]{:S(2)}) collective-permute-start(f32[2,2,64,128]{3,2,1,0:T(8,128)S(1)} %get-tuple-element.16), channel_id=1, source_target_pairs={{0,1},{1,2},{2,3},{3,0},{4,5},{5,6},{6,7},{7,4},{8,9},{9,10},{10,1... | collective-permute-start | bytes 393224 | tf_op jit(solution)/shard_map/ppermute | solution.py:487
  49.0 2.2 %collective-permute-start.9 = (f32[2,2,64,128]{3,2,1,0:T(8,128)S(1)}, f32[2,2,64,128]{3,2,1,0:T(8,128)S(1)}, u32[]{:S(2)}, u32[]{:S(2)}) collective-permute-start(f32[2,2,64,128]{3,2,1,0:T(8,128)S(1)} %get-tuple-element.17), channel_id=1, source_target_pairs={{1,0},{2,1},{3,2},{0,3},{5,4},{6,5},{7,6},{4,7},{9,8},{10,9},{11,1... | collective-permute-start | bytes 393224 | tf_op jit(solution)/shard_map/ppermute | solution.py:486
  51.3 3.7 %collective-permute-done.8.below_ref = f32[2,2,64,128]{3,2,1,0:T(8,128)S(1)} collective-permute-done((f32[2,2,64,128]{3,2,1,0:T(8,128)S(1)}, f32[2,2,64,128]{3,2,1,0:T(8,128)S(1)}, u32[]{:S(2)}, u32[]{:S(2)}) %collective-permute-start.8) | collective-permute-done | bytes 131104 | tf_op jit(solution)/shard_map/ppermute | solution.py:487
  55.0 30.6 %krylov.1 = (f32[7,8,32,256]{3,2,1,0:T(8,128)S(1)}, f32[128,128]{1,0:T(8,128)S(1)}) custom-call(s32[1]{0:T(128)} %bitcast.flip_ref, f32[16,8,32,256]{3,2,1,0:T(8,128)S(1)} %copy-done, f32[2,2,32,80,128]{4,3,2,1,0:T(8,128)S(1)} %get-tuple-element.15.ext_ref, f32[2,2,64,128]{3,2,1,0:T(8,128)S(1)} %collective-permute-done.8.below_ref, ...), custom_call_target="tpu_custom_call" | custom-call | tf_op jit(solution)/shard_map/krylov/pallas_call | solution.py:490
  85.5 18.7 %all_to_all.11 = f32[128,1,128]{2,1,0:T(1,128)S(1)} all-to-all(f32[128,1,128]{2,1,0:T(1,128)S(1)} %bitcast.6), channel_id=1, replica_groups=mesh['y'=4,'xh'=2,'xl'=2,'co'=2,'z'=4] {'y','xh','xl','co','z'}, dimensions={0} | all-to-all | bytes 131072 | tf_op jit(solution)/shard_map/all_to_all | solution.py:500
  104.3 1.2 %combine.1 = (f32[8,32,256]{2,1,0:T(8,128)}, f32[8,32,256]{2,1,0:T(8,128)}) custom-call(f32[128,128]{1,0:T(8,128)S(1)} %bitcast.5, f32[7,8,32,256]{3,2,1,0:T(8,128)S(1)} %get-tuple-element.19.vectors_ref), custom_call_target="tpu_custom_call" | custom-call | tf_op jit(solution)/shard_map/combine/pallas_call | solution.py:502
  (10 shorter events, 0.1 us)
Async XLA Ops:
  0.6 54.4 %copy-start = (f32[16,8,32,256]{3,2,1,0:T(8,128)S(1)}, f32[16,8,32,256]{3,2,1,0:T(8,128)}, u32[]{:S(2)}) copy-start(f32[16,8,32,256]{3,2,1,0:T(8,128)} %sketch_hbm.1) | copy-start | bytes 12582916
  0.6 1.1 %copy-start.1 = (f32[8,32,256]{2,1,0:T(8,128)S(1)}, f32[8,32,256]{2,1,0:T(8,128)}, u32[]{:S(2)}) copy-start(f32[8,32,256]{2,1,0:T(8,128)} %rhs_ref.1) | copy-start | bytes 786436
  1.7 1.2 %copy-start.2 = (f32[8,32,256]{2,1,0:T(8,128)S(1)}, f32[8,32,256]{2,1,0:T(8,128)}, u32[]{:S(2)}) copy-start(f32[8,32,256]{2,1,0:T(8,128)} %coef_ref.1) | copy-start | bytes 786436
  3.0 14.9 %collective-permute-start = (f32[2,8,32,256]{3,2,1,0:T(8,128)S(1)}, f32[2,8,32,256]{3,2,1,0:T(8,128)S(1)}, u32[]{:S(2)}, u32[]{:S(2)}) collective-permute-start(f32[2,8,32,256]{3,2,1,0:T(8,128)S(1)} %prep.1.refs_0_), channel_id=1, source_target_pairs={{0,16},{16,0},{1,17},{17,1},{2,18},{18,2},{3,19},{19,3},{4,20},{20... | collective-permute-start | bytes 1572872 | tf_op jit(solution)/shard_map/ppermute | solution.py:455
  17.9 19.5 %collective-permute-start.1 = (f32[2,8,32,256]{3,2,1,0:T(8,128)S(1)}, f32[2,8,32,256]{3,2,1,0:T(8,128)S(1)}, u32[]{:S(2)}, u32[]{:S(2)}) collective-permute-start(f32[2,8,32,256]{3,2,1,0:T(8,128)S(1)} %collective-permute-done.refs_1_), channel_id=1, source_target_pairs={{0,32},{16,112},{32,64},{48,16},{64,96},{80,48},{96,0},{112,80},{1... | collective-permute-start | bytes 1572872 | tf_op jit(solution)/shard_map/ppermute | solution.py:458
  19.5 6.1 %collective-permute-start.3 = (f32[2,4,32,256]{3,2,1,0:T(8,128)S(1)}, f32[2,4,32,256]{3,2,1,0:T(8,128)S(1)}, u32[]{:S(2)}, u32[]{:S(2)}) collective-permute-start(f32[2,4,32,256]{3,2,1,0:T(8,128)S(1)} %get-tuple-element.20), channel_id=1, source_target_pairs={{32,0},{112,16},{64,32},{16,48},{96,64},{48,80},{0,96},{80,112},{3... | collective-permute-start | bytes 786440 | tf_op jit(solution)/shard_map/ppermute | solution.py:457
  21.0 16.3 %collective-permute-start.2 = (f32[2,4,32,256]{3,2,1,0:T(8,128)S(1)}, f32[2,4,32,256]{3,2,1,0:T(8,128)S(1)}, u32[]{:S(2)}, u32[]{:S(2)}) collective-permute-start(f32[2,4,32,256]{3,2,1,0:T(8,128)S(1)} %get-tuple-element.21), channel_id=1, source_target_pairs={{0,32},{16,112},{32,64},{48,16},{64,96},{80,48},{96,0},{112,80},{1... | collective-permute-start | bytes 786440 | tf_op jit(solution)/shard_map/ppermute | solution.py:456
  21.1 19.5 %collective-permute-start.4 = (f32[2,22,8,256]{3,2,1,0:T(8,128)S(1)}, f32[2,22,8,256]{3,2,1,0:T(8,128)S(1)}, u32[]{:S(2)}, u32[]{:S(2)}) collective-permute-start(f32[2,22,8,256]{3,2,1,0:T(8,128)S(1)} %get-tuple-element.11), channel_id=1, source_target_pairs={{0,4},{4,8},{8,12},{12,0},{1,5},{5,9},{9,13},{13,1},{2,6},{6,10},{... | collective-permute-start | bytes 1081352 | tf_op jit(solution)/shard_map/ppermute | solution.py:471
  24.6 16.0 %collective-permute-start.5 = (f32[2,22,8,256]{3,2,1,0:T(8,128)S(1)}, f32[2,22,8,256]{3,2,1,0:T(8,128)S(1)}, u32[]{:S(2)}, u32[]{:S(2)}) collective-permute-start(f32[2,22,8,256]{3,2,1,0:T(8,128)S(1)} %get-tuple-element.12), channel_id=1, source_target_pairs={{4,0},{8,4},{12,8},{0,12},{5,1},{9,5},{13,9},{1,13},{6,2},{10,6},{... | collective-permute-start | bytes 1081352 | tf_op jit(solution)/shard_map/ppermute | solution.py:470
  37.3 7.5 %collective-permute-start.6 = (f32[2,13,8,256]{3,2,1,0:T(8,128)S(1)}, f32[2,13,8,256]{3,2,1,0:T(8,128)S(1)}, u32[]{:S(2)}, u32[]{:S(2)}) collective-permute-start(f32[2,13,8,256]{3,2,1,0:T(8,128)S(1)} %get-tuple-element.13), channel_id=1, source_target_pairs={{0,4},{4,8},{8,12},{12,0},{1,5},{5,9},{9,13},{13,1},{2,6},{6,10},{... | collective-permute-start | bytes 638984 | tf_op jit(solution)/shard_map/ppermute | solution.py:471
  40.6 5.8 %collective-permute-start.7 = (f32[2,13,8,256]{3,2,1,0:T(8,128)S(1)}, f32[2,13,8,256]{3,2,1,0:T(8,128)S(1)}, u32[]{:S(2)}, u32[]{:S(2)}) collective-permute-start(f32[2,13,8,256]{3,2,1,0:T(8,128)S(1)} %get-tuple-element.14), channel_id=1, source_target_pairs={{4,0},{8,4},{12,8},{0,12},{5,1},{9,5},{13,9},{1,13},{6,2},{10,6},{... | collective-permute-start | bytes 638984 | tf_op jit(solution)/shard_map/ppermute | solution.py:470
  47.3 7.6 %collective-permute-start.8 = (f32[2,2,64,128]{3,2,1,0:T(8,128)S(1)}, f32[2,2,64,128]{3,2,1,0:T(8,128)S(1)}, u32[]{:S(2)}, u32[]{:S(2)}) collective-permute-start(f32[2,2,64,128]{3,2,1,0:T(8,128)S(1)} %get-tuple-element.16), channel_id=1, source_target_pairs={{0,1},{1,2},{2,3},{3,0},{4,5},{5,6},{6,7},{7,4},{8,9},{9,10},{10,1... | collective-permute-start | bytes 393224 | tf_op jit(solution)/shard_map/ppermute | solution.py:487
  49.0 5.9 %collective-permute-start.9 = (f32[2,2,64,128]{3,2,1,0:T(8,128)S(1)}, f32[2,2,64,128]{3,2,1,0:T(8,128)S(1)}, u32[]{:S(2)}, u32[]{:S(2)}) collective-permute-start(f32[2,2,64,128]{3,2,1,0:T(8,128)S(1)} %get-tuple-element.17), channel_id=1, source_target_pairs={{1,0},{2,1},{3,2},{0,3},{5,4},{6,5},{7,6},{4,7},{9,8},{10,9},{11,1... | collective-permute-start | bytes 393224 | tf_op jit(solution)/shard_map/ppermute | solution.py:486
where the time goes:
time: 106 us
  waiting for transfers between devices  33.4 us (32%)
  Pallas kernels  32.8 us (31%)
  blocking collectives  18.7 us (18%)
  starting transfers between devices  17.5 us (17%)
  local copies, waits for them, and re-layouts  2.31 us (2%)
    pallas_call x1, Pallas kernels, local(): pl.pallas_call(main_kernel, out_shape=[struct(7, BX, BY, BZ), struct(128,...  30.6 us
    all_to_all x1, blocking collectives, local(): lax.all_to_all(images, ('y', 'xh', 'xl', 'co', 'z'), 0, 0, tiled=True)  18.7 us
    ppermute x1, waiting for transfers between devices, local(): outer_relay = lax.ppermute(block[:, 4:], ('y', 'xh'), pairs)  11.7 us
    ppermute x1, waiting for transfers between devices, local(): twin = lax.ppermute(block, 'xh', [(0, 1), (1, 0)])  11.2 us
    ppermute x2, starting transfers between devices, pack(): below = lax.ppermute(high, ('xl', 'co'), around)  6.81 us
    ppermute x2, waiting for transfers between devices, pack(): below = lax.ppermute(high, ('xl', 'co'), around)  4.23 us
    ppermute x1, waiting for transfers between devices, local(): below = lax.ppermute(high, 'z', around)  3.73 us
    ppermute x1, starting transfers between devices, local(): twin = lax.ppermute(block, 'xh', [(0, 1), (1, 0)])  3.64 us
  transfers between devices with their start and end apart: 10, of which 6 were waited for; matrix products, arithmetic and copies ran while one was open for 0% of the time, Pallas kernels for 0%

commit v1 on v0

v1 whole, which is shorter than its diff:
```python
import functools

import jax
import jax.numpy as jnp
from jax import lax
from jax.experimental import pallas as pl
from jax.experimental.pallas import tpu as pltpu
from jax.sharding import Mesh
from jax.sharding import PartitionSpec as P

SK = 16
SWEEPS = 3
ITERS = 3
RADIUS = 4
DEPTH = ITERS * RADIUS
BX, BY, BZ = 8, 32, 256
ROW0 = 24
ROWS = 80
LAYERS = BX + 2 * DEPTH
OWN = DEPTH

VMEM = pltpu.VMEM
F32 = jnp.float32


def layer_of(part, idx):
    if part == "own":
        return OWN + idx
    if part == "twin":
        return OWN + 15 - idx
    if part == "relay":
        return OWN - 1 - idx
    if part == "outer_relay":
        return idx
    return OWN + 16 + idx


def distance(layer):
    return max(0, OWN - layer, layer - (OWN + BX - 1))


ALL_PARTS = (
    [("outer_relay", i) for i in range(4)]
    + [("relay", i) for i in range(8)]
    + [("own", i) for i in range(8)]
    + [("twin", i) for i in range(8)]
    + [("outer_twin", i) for i in range(4)]
)

FIRST = (
    [("A", ("own", i)) for i in range(8)]
    + [("A", ("twin", i)) for i in range(8)]
    + [("B", ("own", i), ("own", i + 1)) for i in (0, 2, 4, 6)]
    + [("B", ("twin", i), ("twin", i + 1)) for i in (4, 6)]
)
SECOND = (
    [("A", ("relay", i)) for i in range(8)]
    + [("B", ("relay", i), ("relay", i + 1)) for i in (0, 2)]
    + [
        ("C", ("outer_relay", 1), ("outer_relay", 2)),
        ("C", ("outer_relay", 3), ("outer_twin", 0)),
        ("C", ("outer_twin", 1), ("outer_twin", 2)),
    ]
)


def lane_plan():
    plan = {}
    for tile, dists in enumerate((range(2), range(2, DEPTH))):
        order = [part for part in ALL_PARTS if distance(layer_of(*part)) in dists]
        order.sort(key=lambda part: -distance(layer_of(*part)))
        place, before = 0, 0
        for part in order:
            width = DEPTH - distance(layer_of(*part))
            place += max(width, before)
            before = width
            plan[part] = (tile, place, width)
        first = DEPTH - distance(layer_of(*order[0]))
        assert place + max(before, first) - first <= 128
    return plan


LANES = lane_plan()


def roll(value, shift, axis):
    shift = shift % value.shape[axis]
    if shift == 0:
        return value
    return pltpu.roll(value, shift, axis)


def prep_kernel(flip_ref, rhs_ref, coef_ref, out_ref):
    flip = flip_ref[0]
    for i in range(BX):
        source = jnp.where(flip == 1, BX - 1 - i, i)
        out_ref[0, i] = rhs_ref[source]
        out_ref[1, i] = 1.0 / (6.0 + coef_ref[source])


def pack_rows_kernel(slots, names, *refs):
    sources = dict(zip(names, refs))
    low_ref, high_ref = refs[len(names) :]
    sub = lax.broadcasted_iota(jnp.int32, (8, BZ), 0)
    for array in range(2):
        for slot, (kind, *parts) in enumerate(slots):
            values = []
            for tiles in ((0, 1), (3, 2)):
                tile = tiles[1] if kind == "B" else tiles[0]
                values.append([sources[p][array, i, tile * 8 : tile * 8 + 8] for p, i in parts])
            low, high = values
            if kind == "A":
                low_ref[array, slot] = low[0]
                high_ref[array, slot] = high[0]
            else:
                low_ref[array, slot] = jnp.where(sub < 4, low[0], roll(low[1], 4, 0))
                high_ref[array, slot] = jnp.where(sub >= 4, high[0], roll(high[1], 4, 0))


def row_sources(slots):
    found = {}
    for slot, (kind, *parts) in enumerate(slots):
        for at, part in enumerate(parts):
            below, above = (0, 7) if kind == "B" else (1, 6)
            found.setdefault(part, {})[below] = (slot, at)
            found.setdefault(part, {})[above] = (slot, at)
    return found


def halo_tile(message_ref, array, where, lane_tile):
    slot, rolled = where
    value = message_ref[array, slot, :, lane_tile * 128 : lane_tile * 128 + 128]
    return roll(value, 4, 0) if rolled else value


PART_NAMES = ("own", "twin", "relay", "outer_relay", "outer_twin")
FOUND = (row_sources(FIRST), row_sources(SECOND))


class Blocks:
    def __init__(self, refs):
        self.sources = dict(zip(PART_NAMES, refs[:5]))
        self.below = (refs[5], refs[7])
        self.above = (refs[6], refs[8])

    def tile(self, array, part, row_tile, lane_tile):
        cols = slice(lane_tile * 128, lane_tile * 128 + 128)
        if 2 <= row_tile <= 5:
            name, idx = part
            return self.sources[name][array, idx, row_tile * 8 - 16 : row_tile * 8 - 8, cols]
        message = 0 if part in FOUND[0] else 1
        where = FOUND[message].get(part, {}).get(row_tile)
        if where is None:
            return None
        side = self.below if row_tile < 2 else self.above
        return halo_tile(side[message], array, where, lane_tile)


def pack_columns_kernel(*refs):
    blocks = Blocks(refs)
    low_ref, high_ref = refs[9:]
    lane = lax.broadcasted_iota(jnp.int32, (8, 128), 1)
    for array in range(2):
        for row_tile in range(8):
            low, high = [None, None], [None, None]
            for part, (tile, place, width) in LANES.items():
                first = blocks.tile(array, part, row_tile, 0)
                if first is None:
                    continue
                value = roll(first, place + 64, 1)
                start = (place + 64) % 128
                if start + width <= 128:
                    mask = (lane >= start) & (lane < start + width)
                else:
                    mask = (lane >= start) | (lane < start + width - 128)
                low[tile] = value if low[tile] is None else jnp.where(mask, value, low[tile])
                value = roll(blocks.tile(array, part, row_tile, 1), place, 1)
                mask = (lane >= place - width) & (lane < place)
                high[tile] = value if high[tile] is None else jnp.where(mask, value, high[tile])
            for tile in range(2):
                for value, out_ref in ((low[tile], low_ref), (high[tile], high_ref)):
                    if value is not None:
                        out_ref[array, tile, row_tile * 8 : row_tile * 8 + 8] = value


def rows_of(reach):
    if reach == 0:
        return range(2, 6)
    return range(1, 7) if reach <= 8 else range(0, 8)


def over_layers(first, count, group, body):
    whole, rest = divmod(count, group)

    def step(i, _):
        body(first + i * group, group)
        return 0

    if whole == 1:
        body(first, group)
    elif whole > 1:
        lax.fori_loop(0, whole, step, 0)
    if rest:
        body(first + whole * group, rest)


def neighbour_sums(ref, layer, count, row, tiles, lane, out):
    here = {(l, t): ref[t, layer + l, row : row + 8] for l in range(-1, count + 1) for t in range(tiles)}
    for l in range(count):
        ups = [roll(here[l, t], 127, 1) for t in range(tiles)]
        downs = [roll(here[l, t], 1, 1) for t in range(tiles)]
        if tiles == 2:
            ups = [jnp.where(lane == 127, ups[1 - t], ups[t]) for t in range(2)]
            downs = [jnp.where(lane == 0, downs[1 - t], downs[t]) for t in range(2)]
        for t in range(tiles):
            total = here[l - 1, t] + here[l + 1, t]
            total = total + (ref[t, layer + l, row - 1 : row + 7] + ref[t, layer + l, row + 1 : row + 9])
            out(l, t, here[l, t], total + (ups[t] + downs[t]))


def krylov_steps(vec, inv, za, zb, mid, tiles, group, lane, keep_own):
    for step in range(ITERS):
        reach = DEPTH - step * RADIUS

        def sweep(source, target, left, keep):
            def body(layer, count):
                for row_tile in rows_of(left):
                    row = 8 + row_tile * 8

                    def out(l, t, here, total):
                        total = total + vec[t, layer + l, row : row + 8]
                        if keep:
                            mid[t, layer + l, row : row + 8] = total
                        target[t, layer + l, row : row + 8] = total * inv[t, layer + l, row : row + 8]

                    neighbour_sums(source, layer, count, row, tiles, lane, out)

            over_layers(OWN - left, BX + 2 * left, group, body)

        sweep(za, zb, reach - 1, False)
        sweep(zb, za, reach - 2, False)
        sweep(za, zb, reach - 3, True)
        left = reach - 4
        last = step == ITERS - 1

        def apply(layer, count):
            for row_tile in rows_of(left):
                row = 8 + row_tile * 8

                def out(l, t, here, total):
                    value = 12.0 * here - mid[t, layer + l, row : row + 8] - total
                    vec[t, layer + l, row : row + 8] = value
                    if not last:
                        za[t, layer + l, row : row + 8] = value * inv[t, layer + l, row : row + 8]

                neighbour_sums(zb, layer, count, row, tiles, lane, out)

        over_layers(OWN - left, BX + 2 * left, group, apply)
        keep_own(step)


def sketch_sums(sums_ref, start_ref, sketch_ref, field_of, first, width):
    group = 4
    fields = range(first, 4)
    for start in range(0, SK, group):

        def body(i, carry):
            carry = list(carry)
            for row in range(0, BY, 8):
                for t in range(width):
                    cols = slice(t * 128, t * 128 + 128)
                    values = [field_of(j, i, row, t) for j in fields]
                    for s in range(group):
                        weight = sketch_ref[start + s, i, row : row + 8, cols]
                        for j, value in enumerate(values):
                            carry[j * group + s] = carry[j * group + s] + weight * value
            return tuple(carry)

        at = [(j * SK + start + s) for j in fields for s in range(group)]
        if start_ref is None:
            zero = jnp.zeros((8, 128), F32)
            init = (zero,) * len(at)
        else:
            init = tuple(start_ref[k] for k in at)
        for k, value in zip(at, lax.fori_loop(0, BX, body, init)):
            sums_ref[k] = value


def interior_kernel(flip_ref, sketch, *refs):
    blocks = Blocks(refs[:9])
    vectors_ref, sums_ref, edge_ref, thin_ref, vec, inv, za, zb, mid = refs[9:]
    flip = flip_ref[0]
    lane = lax.broadcasted_iota(jnp.int32, (8, 128), 1)

    for part in ALL_PARTS:
        layer = layer_of(*part)
        for row_tile in range(8):
            row = 8 + row_tile * 8
            if blocks.tile(0, part, row_tile, 0) is None:
                continue
            values = [[blocks.tile(array, part, row_tile, t) for t in range(2)] for array in range(2)]
            for t in range(2):
                vec[t, layer, row : row + 8] = values[0][t]
                inv[t, layer, row : row + 8] = values[1][t]
                za[t, layer, row : row + 8] = values[0][t] * values[1][t]
            for array in range(2):
                edge_ref[array, layer, row : row + 8] = jnp.where(
                    lane < 32, values[array][0], roll(values[array][1], 64, 1)
                )

    def natural(i):
        return jnp.where(flip == 1, BX - 1 - i, i)

    def own(source, place):
        def body(i, _):
            for row in range(0, BY, 8):
                for t in range(2):
                    vectors_ref[place, natural(i), row : row + 8, t * 128 : t * 128 + 128] = source[
                        t, OWN + i, ROW0 + row : ROW0 + row + 8
                    ]
            return 0

        lax.fori_loop(0, BX, body, 0)

    own(vec, 0)

    def keep_own(step):
        own(vec, 1 + step)
        own(zb, 4 + step)

    krylov_steps(vec, inv, za, zb, mid, 2, 2, lane, keep_own)

    def field_of(j, i, row, t):
        value = vectors_ref[j, i, row : row + 8, t * 128 : t * 128 + 128]
        if j == 0:
            return value
        return jnp.where(lane >= DEPTH if t == 0 else lane < 128 - DEPTH, value, 0.0)

    sketch_sums(sums_ref, None, sketch, field_of, 0, 2)

    def thin(i, _):
        for s in range(SK):
            for row in range(0, BY, 8):
                left = sketch[s, i, row : row + 8, 0:128]
                right = roll(sketch[s, i, row : row + 8, 128:256], 64, 1)
                thin_ref[s, i, row : row + 8] = jnp.where(lane < 32, left, right)
        return 0

    lax.fori_loop(0, BX, thin, 0)


def edge_kernel(flip_ref, edge_ref, below_ref, above_ref, thin_ref, before_ref, vectors_ref, images_ref, vec, inv, za, zb, mid, sums):
    flip = flip_ref[0]
    lane = lax.broadcasted_iota(jnp.int32, (8, 128), 1)

    for part, (tile, place, width) in LANES.items():
        layer = layer_of(*part)
        mask = (lane >= place - width) & (lane < place)
        for row_tile in rows_of(DEPTH) if distance(layer) <= 3 else rows_of(8):
            at = slice(8 + row_tile * 8, 16 + row_tile * 8)
            values = []
            for array in range(2):
                rows = slice(row_tile * 8, row_tile * 8 + 8)
                halo = jnp.where(mask, below_ref[array, tile, rows], above_ref[array, tile, rows])
                values.append(jnp.where(lane < 64, edge_ref[array, layer, at], roll(halo, -place, 1)))
            vec[0, layer, at] = values[0]
            inv[0, layer, at] = values[1]
            za[0, layer, at] = values[0] * values[1]

    def natural(i):
        return jnp.where(flip == 1, BX - 1 - i, i)

    def own(source, place):
        def body(i, _):
            for row in range(0, BY, 8):
                vectors_ref[place, natural(i), row : row + 8] = source[0, OWN + i, ROW0 + row : ROW0 + row + 8]
            return 0

        lax.fori_loop(0, BX, body, 0)

    own(vec, 0)

    def keep_own(step):
        own(vec, 1 + step)
        own(zb, 4 + step)

    krylov_steps(vec, inv, za, zb, mid, 1, 6, lane, keep_own)

    inside = (lane < DEPTH) | ((lane >= 64 - DEPTH) & (lane < 64))

    def field_of(j, i, row, t):
        return jnp.where(inside, vectors_ref[j, i, row : row + 8], 0.0)

    sketch_sums(sums, before_ref, thin_ref, field_of, 1, 1)
    lanes = lax.broadcasted_iota(jnp.int32, (1, 128), 1)
    image = jnp.zeros((1, 128), F32)
    for k in range(4 * SK):
        value = sums[k] if k >= SK else before_ref[k]
        value = jnp.sum(jnp.sum(value, axis=0, keepdims=True), axis=1, keepdims=True)
        image = jnp.where(lanes == k, value, image)
    images_ref[...] = jnp.broadcast_to(image, images_ref.shape)


def dot(left, right):
    return jnp.sum(left * right, axis=0, keepdims=True)


def small_solve(totals):
    row = lax.broadcasted_iota(jnp.int32, (4 * SK, 128), 0)
    col = lax.broadcasted_iota(jnp.int32, (4 * SK, 128), 1)
    wide = jnp.where(row == col, jnp.broadcast_to(totals, (4 * SK, 128)), 0.0)
    spread = jnp.broadcast_to(jnp.sum(wide, axis=1, keepdims=True), (4 * SK, 128))
    sketches = [spread[j * SK : (j + 1) * SK] for j in range(4)]
    zero = jnp.zeros((1, 128), F32)
    beta = jnp.sqrt(dot(sketches[0], sketches[0]))
    basis = [[1.0 / beta, zero, zero, zero]]
    images = [sketches[0] / beta]
    hessen = [[zero] * ITERS for _ in range(ITERS + 1)]
    for j in range(ITERS):
        combo = [zero] + [basis[j][i] for i in range(3)]
        image = combo[1] * sketches[1]
        for i in range(1, j + 1):
            image = image + combo[i + 1] * sketches[i + 1]
        weights = [dot(member, image) for member in images]
        rest = image
        for i in range(j + 1):
            rest = rest - weights[i] * images[i]
            combo = [combo[k] - weights[i] * basis[i][k] for k in range(4)]
            hessen[i][j] = weights[i]
        length = jnp.sqrt(dot(rest, rest))
        hessen[j + 1][j] = length
        basis.append([entry / length for entry in combo])
        images.append(rest / length)
    target = [beta, zero, zero, zero]

    def inner(left, right):
        total = left[0] * right[0]
        for a, b in zip(left[1:], right[1:]):
            total = total + a * b
        return total

    members = []
    upper = [[None] * ITERS for _ in range(ITERS)]
    for j in range(ITERS):
        column = [hessen[i][j] for i in range(ITERS + 1)]
        for i in range(j):
            factor = inner(members[i], column)
            upper[i][j] = factor
            column = [c - factor * m for c, m in zip(column, members[i])]
        diag = jnp.sqrt(inner(column, column))
        upper[j][j] = diag
        members.append([c / diag for c in column])
    coeffs = [None] * ITERS
    for j in reversed(range(ITERS)):
        accum = inner(members[j], target)
        for i in range(j + 1, ITERS):
            accum = accum - upper[j][i] * coeffs[i]
        coeffs[j] = accum / upper[j][j]
    leftover = []
    for i in range(ITERS + 1):
        total = hessen[i][0] * coeffs[0]
        for j in range(1, ITERS):
            total = total + hessen[i][j] * coeffs[j]
        leftover.append(target[i] - total)
    for_images = []
    for i in range(ITERS):
        total = coeffs[0] * basis[0][i]
        for j in range(1, ITERS):
            total = total + coeffs[j] * basis[j][i]
        for_images.append(total)
    for_vectors = []
    for i in range(ITERS + 1):
        total = leftover[0] * basis[0][i]
        for j in range(1, ITERS + 1):
            total = total + leftover[j] * basis[j][i]
        for_vectors.append(total)
    return for_images, for_vectors


def final_kernel(sums_ref, vectors_ref, edges_ref, solution_ref, residual_ref):
    totals = jnp.sum(sums_ref[...], axis=0, keepdims=True)
    for_images, for_vectors = small_solve(totals)
    for_images = [jnp.broadcast_to(w, (8, 128)) for w in for_images]
    for_vectors = [jnp.broadcast_to(w, (8, 128)) for w in for_vectors]
    lane = lax.broadcasted_iota(jnp.int32, (8, 128), 1)

    def combined(ref, at):
        image = for_images[0] * ref[(4, *at)]
        for j in range(1, ITERS):
            image = image + for_images[j] * ref[(4 + j, *at)]
        vector = for_vectors[0] * ref[(0, *at)]
        for j in range(1, ITERS + 1):
            vector = vector + for_vectors[j] * ref[(j, *at)]
        return image, vector

    def body(i, _):
        for row in range(0, BY, 8):
            rows = slice(row, row + 8)
            edges = combined(edges_ref, (i, rows))
            turned = [roll(value, 64, 1) for value in edges]
            for t in range(2):
                at = (i, rows, slice(t * 128, t * 128 + 128))
                values = combined(vectors_ref, at)
                if t == 0:
                    values = [jnp.where(lane < DEPTH, e, v) for e, v in zip(edges, values)]
                else:
                    values = [jnp.where(lane >= 128 - DEPTH, e, v) for e, v in zip(turned, values)]
                solution_ref[at] = values[0]
                residual_ref[at] = values[1]
        return 0

    lax.fori_loop(0, BX, body, 0)


def vmem(count):
    return [pl.BlockSpec(memory_space=VMEM)] * count


SMEM_SPEC = pl.BlockSpec(memory_space=pltpu.SMEM)


def struct(*shape):
    return jax.ShapeDtypeStruct(shape, F32)


def params(mib):
    return pltpu.CompilerParams(vmem_limit_bytes=mib << 20)


def local(right_side, wavenumber_sq, sketch_matrix):
    flip = lax.axis_index("xh").astype(jnp.int32).reshape(1)
    block = pl.pallas_call(
        prep_kernel,
        out_shape=struct(2, BX, BY, BZ),
        in_specs=[SMEM_SPEC] + vmem(2),
        out_specs=vmem(1)[0],
        compiler_params=params(8),
        name="prep",
    )(flip, right_side, wavenumber_sq)

    pairs = [(y * 2 + h, (y + (1 - 2 * h)) % 4 * 2 + h) for y in range(4) for h in range(2)]
    back = [(b, a) for a, b in pairs]
    around = [(i, (i + 1) % 4) for i in range(4)]
    inverse = [(b, a) for a, b in around]
    twin = lax.ppermute(block, "xh", [(0, 1), (1, 0)])
    outer_relay = lax.ppermute(block[:, 4:], ("y", "xh"), pairs)
    outer_twin = lax.ppermute(block[:, :4], ("y", "xh"), back)
    twin, outer_relay, outer_twin = lax.optimization_barrier((twin, outer_relay, outer_twin))
    relay = lax.ppermute(twin, ("y", "xh"), pairs)

    def pack(slots, names, *parts):
        count = len(slots)
        low, high = pl.pallas_call(
            functools.partial(pack_rows_kernel, slots, names),
            out_shape=[struct(2, count, 8, BZ)] * 2,
            in_specs=vmem(len(parts)),
            out_specs=vmem(2),
            compiler_params=params(8),
            name="pack_rows",
        )(*parts)
        above = lax.ppermute(low, ("xl", "co"), inverse)
        below = lax.ppermute(high, ("xl", "co"), around)
        return below, above

    below_1, above_1 = pack(FIRST, ("own", "twin"), block, twin)
    below_2, above_2 = pack(
        SECOND, ("relay", "outer_relay", "outer_twin"), relay, outer_relay, outer_twin
    )
    parts = (block, twin, relay, outer_relay, outer_twin, below_1, above_1, below_2, above_2)
    low, high = pl.pallas_call(
        pack_columns_kernel,
        out_shape=[struct(2, 2, 64, 128)] * 2,
        in_specs=vmem(9),
        out_specs=vmem(2),
        compiler_params=params(8),
        name="pack_columns",
    )(*parts)
    above = lax.ppermute(low, "z", inverse)
    below = lax.ppermute(high, "z", around)

    def fields(tiles):
        return [VMEM((tiles, LAYERS, ROWS, 128), F32)] * 5

    vectors, sums, edge, thin = pl.pallas_call(
        interior_kernel,
        out_shape=[struct(7, BX, BY, BZ), struct(4 * SK, 8, 128), struct(2, LAYERS, ROWS, 128), struct(SK, BX, BY, 128)],
        in_specs=[SMEM_SPEC] + vmem(10),
        out_specs=vmem(4),
        scratch_shapes=fields(2),
        compiler_params=params(20),
        cost_estimate=pl.CostEstimate(flops=30_000_000, bytes_accessed=1 << 20, transcendentals=0),
        name="interior",
    )(flip, sketch_matrix, *parts)
    edges, images = pl.pallas_call(
        edge_kernel,
        out_shape=[struct(7, BX, BY, 128), struct(128, 128)],
        in_specs=[SMEM_SPEC] + vmem(5),
        out_specs=vmem(2),
        scratch_shapes=fields(1) + [VMEM((4 * SK, 8, 128), F32)],
        compiler_params=params(12),
        name="edge",
    )(flip, edge, below, above, thin, sums)

    totals = lax.all_to_all(images, ("y", "xh", "xl", "co", "z"), 0, 0, tiled=True)
    return tuple(
        pl.pallas_call(
            final_kernel,
            out_shape=[struct(BX, BY, BZ)] * 2,
            in_specs=vmem(3),
            out_specs=vmem(2),
            compiler_params=params(8),
            name="combine",
        )(totals, vectors, edges)
    )


def solution(mesh):
    finer = Mesh(mesh.devices.reshape(4, 2, 2, 2, 4), ("y", "xh", "xl", "co", "z"))
    spec = (("y", "xh"), ("xl", "co"), "z")
    return jax.shard_map(
        local,
        mesh=finer,
        in_specs=(P(*spec), P(*spec), P(None, *spec)),
        out_specs=(P(*spec), P(*spec)),
        check_vma=False,
    )
```

time: 106 us -> 89.7 us (0.85)
  waiting for transfers between devices: 33.4 us -> 23.3 us
  Pallas kernels: 32.8 us -> 28.4 us
  blocking collectives: 18.7 us -> 17 us
    ppermute x1, waiting for transfers between devices: 11.2 us -> 0.55 us  [local(): twin = lax.ppermute(block, 'xh', [(0, 1), (1, 0)])]
    ppermute x1, waiting for transfers between devices: 0.01 us -> 9.17 us  [local(): relay = lax.ppermute(twin, ('y', 'xh'), pairs)]
    ppermute x1, waiting for transfers between devices: 11.7 us -> 3.13 us  [local(): outer_relay = lax.ppermute(block[:, 4:], ('y', 'xh'), pairs)]
    pallas_call x2 -> x3, Pallas kernels: 31.5 us -> 26.5 us  [the longest x1 18 us: local(): pl.pallas_call(interior_kernel, out_shape=[struct(7, BX, BY, BZ), struct(...]
    ppermute x1, waiting for transfers between devices: 3.73 us -> 0.01 us  [local(): below = lax.ppermute(high, 'z', around)]
    ppermute x1, waiting for transfers between devices: 0.99 us -> 4.71 us  [local(): outer_twin = lax.ppermute(block[:, :4], ('y', 'xh'), back)]
    all_to_all x1, blocking collectives: 18.7 us -> 17 us  [local(): lax.all_to_all(images, ('y', 'xh', 'xl', 'co', 'z'), 0, 0, tiled=True)]
    ppermute x1, starting transfers between devices: 1.51 us -> 2.8 us  [local(): outer_twin = lax.ppermute(block[:, :4], ('y', 'xh'), back)]
  transfers between devices with their start and end apart: 10 -> 10, of which waited for: 6 -> 6; matrix products, arithmetic and copies ran while one was open for 0% -> 0% of each run, Pallas kernels for 0% -> 20%
where the time goes in v1:
time: 89.7 us; the launch traced here: 89.5 us
  Pallas kernels  28.4 us (32%)
  waiting for transfers between devices  23.3 us (26%)
  starting transfers between devices  18.2 us (20%)
  blocking collectives  17 us (19%)
  local copies, waits for them, and re-layouts  1.94 us (2%)
    pallas_call x1, Pallas kernels, local(): pl.pallas_call(interior_kernel, out_shape=[struct(7, BX, BY, BZ), struct(...  18 us
    all_to_all x1, blocking collectives, local(): lax.all_to_all(images, ('y', 'xh', 'xl', 'co', 'z'), 0, 0, tiled=True)  17 us
    ppermute x1, waiting for transfers between devices, local(): relay = lax.ppermute(twin, ('y', 'xh'), pairs)  9.17 us
    pallas_call x1, Pallas kernels, local(): pl.pallas_call(edge_kernel, out_shape=[struct(7, BX, BY, 128), struct(128...  7.51 us
    ppermute x2, starting transfers between devices, pack(): below = lax.ppermute(high, ('xl', 'co'), around)  6.25 us
    ppermute x1, waiting for transfers between devices, local(): outer_twin = lax.ppermute(block[:, :4], ('y', 'xh'), back)  4.71 us
    ppermute x2, waiting for transfers between devices, pack(): below = lax.ppermute(high, ('xl', 'co'), around)  4.23 us
    ppermute x1, starting transfers between devices, local(): twin = lax.ppermute(block, 'xh', [(0, 1), (1, 0)])  3.64 us
  transfers between devices with their start and end apart: 10, of which 6 were waited for; matrix products, arithmetic and copies ran while one was open for 0% of the time, Pallas kernels for 20%

profile of v1, /device:TPU:1, one launch (start us, length us, event | category | flops | bytes accessed | tf_op | source)
XLA Modules:
  0.0 89.5 jit_solution(18225313870799185239)
XLA Ops:
  0.6 0.9 %copy-done.1 = f32[8,32,256]{2,1,0:T(8,128)S(1)} copy-done((f32[8,32,256]{2,1,0:T(8,128)S(1)}, f32[8,32,256]{2,1,0:T(8,128)}, u32[]{:S(2)}) %copy-start.1) | copy-done | bytes 262168
  1.6 0.9 %copy-done.2 = f32[8,32,256]{2,1,0:T(8,128)S(1)} copy-done((f32[8,32,256]{2,1,0:T(8,128)S(1)}, f32[8,32,256]{2,1,0:T(8,128)}, u32[]{:S(2)}) %copy-start.2) | copy-done | bytes 262168
  2.6 3.6 %collective-permute-start = (f32[2,8,32,256]{3,2,1,0:T(8,128)S(1)}, f32[2,8,32,256]{3,2,1,0:T(8,128)S(1)}, u32[]{:S(2)}, u32[]{:S(2)}) collective-permute-start(f32[2,8,32,256]{3,2,1,0:T(8,128)S(1)} %prep.1.refs_0_), channel_id=1, source_target_pairs={{0,16},{16,0},{1,17},{17,1},{2,18},{18,2},{3,19},{19,3},{4,20},{20... | collective-permute-start | bytes 1572872 | tf_op jit(solution)/shard_map/ppermute | solution.py:545
  6.3 2.8 %collective-permute-start.2 = (f32[2,4,32,256]{3,2,1,0:T(8,128)S(1)}, f32[2,4,32,256]{3,2,1,0:T(8,128)S(1)}, u32[]{:S(2)}, u32[]{:S(2)}) collective-permute-start(f32[2,4,32,256]{3,2,1,0:T(8,128)S(1)} %get-tuple-element.32), channel_id=1, source_target_pairs={{32,0},{112,16},{64,32},{16,48},{96,64},{48,80},{0,96},{80,112},{3... | collective-permute-start | bytes 786440 | tf_op jit(solution)/shard_map/ppermute | solution.py:547
  9.1 0.0 collective-permute-start.1
  9.1 4.7 %collective-permute-done.2.refs_2_.refs_4_ = f32[2,4,32,256]{3,2,1,0:T(8,128)S(1)} collective-permute-done((f32[2,4,32,256]{3,2,1,0:T(8,128)S(1)}, f32[2,4,32,256]{3,2,1,0:T(8,128)S(1)}, u32[]{:S(2)}, u32[]{:S(2)}) %collective-permute-start.2) | collective-permute-done | bytes 262176 | tf_op jit(solution)/shard_map/ppermute | solution.py:547
  13.8 3.1 %collective-permute-done.1.refs_1_.refs_3_ = f32[2,4,32,256]{3,2,1,0:T(8,128)S(1)} collective-permute-done((f32[2,4,32,256]{3,2,1,0:T(8,128)S(1)}, f32[2,4,32,256]{3,2,1,0:T(8,128)S(1)}, u32[]{:S(2)}, u32[]{:S(2)}) %collective-permute-start.1) | collective-permute-done | bytes 262176 | tf_op jit(solution)/shard_map/ppermute | solution.py:546
  16.9 0.5 collective-permute-done.refs_1_
  17.5 1.6 %collective-permute-start.3 = (f32[2,8,32,256]{3,2,1,0:T(8,128)S(1)}, f32[2,8,32,256]{3,2,1,0:T(8,128)S(1)}, u32[]{:S(2)}, u32[]{:S(2)}) collective-permute-start(f32[2,8,32,256]{3,2,1,0:T(8,128)S(1)} %collective-permute-done.refs_1_), channel_id=1, source_target_pairs={{0,32},{16,112},{32,64},{48,16},{64,96},{80,48},{96,0},{112,80},{1... | collective-permute-start | bytes 1572872 | tf_op jit(solution)/shard_map/ppermute | solution.py:549
  19.1 0.1 pack_rows.2
  19.2 3.0 %collective-permute-start.4 = (f32[2,22,8,256]{3,2,1,0:T(8,128)S(1)}, f32[2,22,8,256]{3,2,1,0:T(8,128)S(1)}, u32[]{:S(2)}, u32[]{:S(2)}) collective-permute-start(f32[2,22,8,256]{3,2,1,0:T(8,128)S(1)} %get-tuple-element.20), channel_id=1, source_target_pairs={{0,4},{4,8},{8,12},{12,0},{1,5},{5,9},{9,13},{13,1},{2,6},{6,10},{... | collective-permute-start | bytes 1081352 | tf_op jit(solution)/shard_map/ppermute | solution.py:562
  22.1 9.2 %collective-permute-done.3.refs_0_.refs_2_ = f32[2,8,32,256]{3,2,1,0:T(8,128)S(1)} collective-permute-done((f32[2,8,32,256]{3,2,1,0:T(8,128)S(1)}, f32[2,8,32,256]{3,2,1,0:T(8,128)S(1)}, u32[]{:S(2)}, u32[]{:S(2)}) %collective-permute-start.3) | collective-permute-done | bytes 524320 | tf_op jit(solution)/shard_map/ppermute | solution.py:549
  31.3 3.3 %collective-permute-start.6 = (f32[2,13,8,256]{3,2,1,0:T(8,128)S(1)}, f32[2,13,8,256]{3,2,1,0:T(8,128)S(1)}, u32[]{:S(2)}, u32[]{:S(2)}) collective-permute-start(f32[2,13,8,256]{3,2,1,0:T(8,128)S(1)} %get-tuple-element.22), channel_id=1, source_target_pairs={{0,4},{4,8},{8,12},{12,0},{1,5},{5,9},{9,13},{13,1},{2,6},{6,10},{... | collective-permute-start | bytes 638984 | tf_op jit(solution)/shard_map/ppermute | solution.py:562
  34.6 0.0 collective-permute-start.7
  34.6 0.0 collective-permute-done.4.refs_5_
  34.6 4.2 %collective-permute-done.6.refs_7_ = f32[2,13,8,256]{3,2,1,0:T(8,128)S(1)} collective-permute-done((f32[2,13,8,256]{3,2,1,0:T(8,128)S(1)}, f32[2,13,8,256]{3,2,1,0:T(8,128)S(1)}, u32[]{:S(2)}, u32[]{:S(2)}) %collective-permute-start.6) | collective-permute-done | bytes 213024 | tf_op jit(solution)/shard_map/ppermute | solution.py:562
  38.8 1.5 %collective-permute-done.7.refs_8_ = f32[2,13,8,256]{3,2,1,0:T(8,128)S(1)} collective-permute-done((f32[2,13,8,256]{3,2,1,0:T(8,128)S(1)}, f32[2,13,8,256]{3,2,1,0:T(8,128)S(1)}, u32[]{:S(2)}, u32[]{:S(2)}) %collective-permute-start.7) | collective-permute-done | bytes 213024 | tf_op jit(solution)/shard_map/ppermute | solution.py:561
  40.4 1.0 %pack_columns.1 = (f32[2,2,64,128]{3,2,1,0:T(8,128)S(1)}, f32[2,2,64,128]{3,2,1,0:T(8,128)S(1)}) custom-call(f32[2,8,32,256]{3,2,1,0:T(8,128)S(1)} %prep.1.refs_0_, f32[2,8,32,256]{3,2,1,0:T(8,128)S(1)} %collective-permute-done.refs_1_, f32[2,8,32,256]{3,2,1,0:T(8,128)S(1)} %collective-permute-done.3.refs_0_.refs_2_, ...), custom_call_target="tpu_custom_call" | custom-call | tf_op jit(solution)/shard_map/pack_columns/pallas_call | solution.py:570
  41.3 1.7 %collective-permute-start.8 = (f32[2,2,64,128]{3,2,1,0:T(8,128)S(1)}, f32[2,2,64,128]{3,2,1,0:T(8,128)S(1)}, u32[]{:S(2)}, u32[]{:S(2)}) collective-permute-start(f32[2,2,64,128]{3,2,1,0:T(8,128)S(1)} %get-tuple-element.25), channel_id=1, source_target_pairs={{0,1},{1,2},{2,3},{3,0},{4,5},{5,6},{6,7},{7,4},{8,9},{9,10},{10,1... | collective-permute-start | bytes 393224 | tf_op jit(solution)/shard_map/ppermute | solution.py:579
  43.0 2.2 %collective-permute-start.9 = (f32[2,2,64,128]{3,2,1,0:T(8,128)S(1)}, f32[2,2,64,128]{3,2,1,0:T(8,128)S(1)}, u32[]{:S(2)}, u32[]{:S(2)}) collective-permute-start(f32[2,2,64,128]{3,2,1,0:T(8,128)S(1)} %get-tuple-element.26), channel_id=1, source_target_pairs={{1,0},{2,1},{3,2},{0,3},{5,4},{6,5},{7,6},{4,7},{9,8},{10,9},{11,1... | collective-permute-start | bytes 393224 | tf_op jit(solution)/shard_map/ppermute | solution.py:578
  45.3 18.0 %interior.1 = (f32[7,8,32,256]{3,2,1,0:T(8,128)S(1)}, f32[64,8,128]{2,1,0:T(8,128)S(1)}, f32[2,32,80,128]{3,2,1,0:T(8,128)S(1)}, f32[16,8,32,128]{3,2,1,0:T(8,128)S(1)}) custom-call(s32[1]{0:T(128)} %bitcast.flip_ref, f32[16,8,32,256]{3,2,1,0:T(8,128)S(1)} %copy-done, f32[2,8,32,256]{3,2,1,0:T(8,128)S(1)} %prep.1.refs_0_, ...), custom_call_target="tpu_custom_call" | custom-call | flops 30000000 | bytes 1048576 | tf_op jit(solution)/shard_map/interior/pallas_call | solution.py:584
  63.3 7.5 %edge.1 = (f32[7,8,32,128]{3,2,1,0:T(8,128)S(1)}, f32[128,128]{1,0:T(8,128)S(1)}) custom-call(s32[1]{0:T(128)} %bitcast.flip_ref, f32[2,32,80,128]{3,2,1,0:T(8,128)S(1)} %get-tuple-element.24.edge_ref, f32[2,2,64,128]{3,2,1,0:T(8,128)S(1)} %collective-permute-done.8.below_ref, f32[2,2,64,128]{3,2,1,0:T(8,128)S(1)} %collective-permute-done.9.above_ref, ...), custom_call_target="tpu_custom_call" | custom-call | tf_op jit(solution)/shard_map/edge/pallas_call | solution.py:594
  70.8 17.0 %all_to_all.11 = f32[128,1,128]{2,1,0:T(1,128)S(1)} all-to-all(f32[128,1,128]{2,1,0:T(1,128)S(1)} %bitcast.6), channel_id=1, replica_groups=mesh['y'=4,'xh'=2,'xl'=2,'co'=2,'z'=4] {'y','xh','xl','co','z'}, dimensions={0} | all-to-all | bytes 131072 | tf_op jit(solution)/shard_map/all_to_all | solution.py:604
  87.8 1.7 %combine.1 = (f32[8,32,256]{2,1,0:T(8,128)}, f32[8,32,256]{2,1,0:T(8,128)}) custom-call(f32[128,128]{1,0:T(8,128)S(1)} %bitcast.5, f32[7,8,32,256]{3,2,1,0:T(8,128)S(1)} %get-tuple-element.30.vectors_ref, f32[7,8,32,128]{3,2,1,0:T(8,128)S(1)} %get-tuple-element.31.edges_ref), custom_call_target="tpu_custom_call" | custom-call | tf_op jit(solution)/shard_map/combine/pallas_call | solution.py:606
  (11 shorter events, 0.1 us)
Async XLA Ops:
  0.6 1.0 %copy-start.1 = (f32[8,32,256]{2,1,0:T(8,128)S(1)}, f32[8,32,256]{2,1,0:T(8,128)}, u32[]{:S(2)}) copy-start(f32[8,32,256]{2,1,0:T(8,128)} %rhs_ref.1) | copy-start | bytes 786436
  1.6 0.9 %copy-start.2 = (f32[8,32,256]{2,1,0:T(8,128)S(1)}, f32[8,32,256]{2,1,0:T(8,128)}, u32[]{:S(2)}) copy-start(f32[8,32,256]{2,1,0:T(8,128)} %coef_ref.1) | copy-start | bytes 786436
  2.6 14.9 %collective-permute-start = (f32[2,8,32,256]{3,2,1,0:T(8,128)S(1)}, f32[2,8,32,256]{3,2,1,0:T(8,128)S(1)}, u32[]{:S(2)}, u32[]{:S(2)}) collective-permute-start(f32[2,8,32,256]{3,2,1,0:T(8,128)S(1)} %prep.1.refs_0_), channel_id=1, source_target_pairs={{0,16},{16,0},{1,17},{17,1},{2,18},{18,2},{3,19},{19,3},{4,20},{20... | collective-permute-start | bytes 1572872 | tf_op jit(solution)/shard_map/ppermute | solution.py:545
  6.3 7.5 %collective-permute-start.2 = (f32[2,4,32,256]{3,2,1,0:T(8,128)S(1)}, f32[2,4,32,256]{3,2,1,0:T(8,128)S(1)}, u32[]{:S(2)}, u32[]{:S(2)}) collective-permute-start(f32[2,4,32,256]{3,2,1,0:T(8,128)S(1)} %get-tuple-element.32), channel_id=1, source_target_pairs={{32,0},{112,16},{64,32},{16,48},{96,64},{48,80},{0,96},{80,112},{3... | collective-permute-start | bytes 786440 | tf_op jit(solution)/shard_map/ppermute | solution.py:547
  9.1 36.2 %copy-start = (f32[16,8,32,256]{3,2,1,0:T(8,128)S(1)}, f32[16,8,32,256]{3,2,1,0:T(8,128)}, u32[]{:S(2)}) copy-start(f32[16,8,32,256]{3,2,1,0:T(8,128)} %sketch.1) | copy-start | bytes 12582916
  9.1 7.8 %collective-permute-start.1 = (f32[2,4,32,256]{3,2,1,0:T(8,128)S(1)}, f32[2,4,32,256]{3,2,1,0:T(8,128)S(1)}, u32[]{:S(2)}, u32[]{:S(2)}) collective-permute-start(f32[2,4,32,256]{3,2,1,0:T(8,128)S(1)} %get-tuple-element.33), channel_id=1, source_target_pairs={{0,32},{16,112},{32,64},{48,16},{64,96},{80,48},{96,0},{112,80},{1... | collective-permute-start | bytes 786440 | tf_op jit(solution)/shard_map/ppermute | solution.py:546
  17.5 13.8 %collective-permute-start.3 = (f32[2,8,32,256]{3,2,1,0:T(8,128)S(1)}, f32[2,8,32,256]{3,2,1,0:T(8,128)S(1)}, u32[]{:S(2)}, u32[]{:S(2)}) collective-permute-start(f32[2,8,32,256]{3,2,1,0:T(8,128)S(1)} %collective-permute-done.refs_1_), channel_id=1, source_target_pairs={{0,32},{16,112},{32,64},{48,16},{64,96},{80,48},{96,0},{112,80},{1... | collective-permute-start | bytes 1572872 | tf_op jit(solution)/shard_map/ppermute | solution.py:549
  19.2 15.5 %collective-permute-start.4 = (f32[2,22,8,256]{3,2,1,0:T(8,128)S(1)}, f32[2,22,8,256]{3,2,1,0:T(8,128)S(1)}, u32[]{:S(2)}, u32[]{:S(2)}) collective-permute-start(f32[2,22,8,256]{3,2,1,0:T(8,128)S(1)} %get-tuple-element.20), channel_id=1, source_target_pairs={{0,4},{4,8},{8,12},{12,0},{1,5},{5,9},{9,13},{13,1},{2,6},{6,10},{... | collective-permute-start | bytes 1081352 | tf_op jit(solution)/shard_map/ppermute | solution.py:562
  22.1 12.5 %collective-permute-start.5 = (f32[2,22,8,256]{3,2,1,0:T(8,128)S(1)}, f32[2,22,8,256]{3,2,1,0:T(8,128)S(1)}, u32[]{:S(2)}, u32[]{:S(2)}) collective-permute-start(f32[2,22,8,256]{3,2,1,0:T(8,128)S(1)} %get-tuple-element.21), channel_id=1, source_target_pairs={{4,0},{8,4},{12,8},{0,12},{5,1},{9,5},{13,9},{1,13},{6,2},{10,6},{... | collective-permute-start | bytes 1081352 | tf_op jit(solution)/shard_map/ppermute | solution.py:561
  31.3 7.5 %collective-permute-start.6 = (f32[2,13,8,256]{3,2,1,0:T(8,128)S(1)}, f32[2,13,8,256]{3,2,1,0:T(8,128)S(1)}, u32[]{:S(2)}, u32[]{:S(2)}) collective-permute-start(f32[2,13,8,256]{3,2,1,0:T(8,128)S(1)} %get-tuple-element.22), channel_id=1, source_target_pairs={{0,4},{4,8},{8,12},{12,0},{1,5},{5,9},{9,13},{13,1},{2,6},{6,10},{... | collective-permute-start | bytes 638984 | tf_op jit(solution)/shard_map/ppermute | solution.py:562
  34.6 5.8 %collective-permute-start.7 = (f32[2,13,8,256]{3,2,1,0:T(8,128)S(1)}, f32[2,13,8,256]{3,2,1,0:T(8,128)S(1)}, u32[]{:S(2)}, u32[]{:S(2)}) collective-permute-start(f32[2,13,8,256]{3,2,1,0:T(8,128)S(1)} %get-tuple-element.23), channel_id=1, source_target_pairs={{4,0},{8,4},{12,8},{0,12},{5,1},{9,5},{13,9},{1,13},{6,2},{10,6},{... | collective-permute-start | bytes 638984 | tf_op jit(solution)/shard_map/ppermute | solution.py:561
  41.3 21.9 %collective-permute-start.8 = (f32[2,2,64,128]{3,2,1,0:T(8,128)S(1)}, f32[2,2,64,128]{3,2,1,0:T(8,128)S(1)}, u32[]{:S(2)}, u32[]{:S(2)}) collective-permute-start(f32[2,2,64,128]{3,2,1,0:T(8,128)S(1)} %get-tuple-element.25), channel_id=1, source_target_pairs={{0,1},{1,2},{2,3},{3,0},{4,5},{5,6},{6,7},{7,4},{8,9},{9,10},{10,1... | collective-permute-start | bytes 393224 | tf_op jit(solution)/shard_map/ppermute | solution.py:579
  43.0 20.3 %collective-permute-start.9 = (f32[2,2,64,128]{3,2,1,0:T(8,128)S(1)}, f32[2,2,64,128]{3,2,1,0:T(8,128)S(1)}, u32[]{:S(2)}, u32[]{:S(2)}) collective-permute-start(f32[2,2,64,128]{3,2,1,0:T(8,128)S(1)} %get-tuple-element.26), channel_id=1, source_target_pairs={{1,0},{2,1},{3,2},{0,3},{5,4},{6,5},{7,6},{4,7},{9,8},{10,9},{11,1... | collective-permute-start | bytes 393224 | tf_op jit(solution)/shard_map/ppermute | solution.py:578
